TPU v7x, 256 devices: a whole 4x4x8 slice. The times are simulated.
256 devices in a mesh: grp: 8 (over x_hi, y), row: 32 (over z, x_lo, core).
Axes of the slice: x: 4 (x_hi: 2, x_lo: 2; x = x_hi * 2 + x_lo), y: 4, z: 8, core: 2. Of those that a mesh axis runs over, the one named last changes fastest.
Arguments:
- tables: bfloat16 [8, 32768, 512], P(None, 'row', 'grp'), may hold values from -1.1953125 to 1.1953125
- indices: int32 [4096, 8, 32], P('row', 'grp'), may hold values from 0 to 32767
- block_shift: int32 [8], replicated, may hold values from 0 to 31
- pooled_grad: bfloat16 [4096, 8, 512], P('row', 'grp'), may hold values from -6 to 6
Outputs:
- pooled: bfloat16 [4096, 8, 512], P('row', 'grp')
- updated: bfloat16 [8, 32768, 512], P('grp', 'row')
All inputs are finite; a program needn't handle non-finite values.
Results may differ from a plain program's by a relative error of at most 0.001.
Values may be sent and summed in bfloat16 or wider, within the bound.
No kernel may reach another device: no remote copies, remote signals or barrier semaphores. Data moves between devices by JAX's collectives and lax.ppermute only.
A program may use at most 64 MiB of HBM per device.

v0:
```python
import functools

import jax
import jax.numpy as jnp
from jax import lax
from jax.experimental import pallas as pl
from jax.experimental.pallas import tpu as pltpu
from jax.sharding import Mesh, PartitionSpec as P


STEP_RATE = 0.25
ROW = ("z", "xl", "core")
BLOCK = 1024
PIECE = 32
WINDOW = 256
STATIC_HITS = 4


def pool_key(ids, where_ref):
    near = ((ids >> 10) & 3) ^ where_ref[1]
    return jnp.where((ids >> 12) == where_ref[0], (near << 10) | (ids & 1023), -1)


def update_key(ids, where_ref):
    place = ((ids >> 10) + where_ref[2]) & 31
    return jnp.where(((ids >> 5) & 31) == 4 * where_ref[0] + where_ref[1], (place << 5) | (ids & 31), -1)


def count_kernel(key_of, where_ref, ids_ref, out_ref, keys_ref, hits_ref):
    owners = out_ref.shape[0]
    windows = out_ref.shape[1] // WINDOW
    bag, _, lanes = keys_ref.shape
    for k in range(bag):
        keys_ref[k] = key_of(ids_ref[pl.ds(k, owners, stride=bag), :], where_ref)
    most = jnp.zeros((owners, lanes), jnp.int32)
    for w in range(windows):
        window = pl.program_id(1) * windows + w
        hits = []
        total = jnp.zeros((owners, lanes), jnp.int32)
        for k in range(bag):
            key = keys_ref[k]
            mine = (key >> 8) == window
            hits.append(jnp.full((owners, lanes), -1, jnp.int32))
            for j in range(k, 0, -1):
                hits[j] = jnp.where(mine, hits[j - 1], hits[j])
            hits[0] = jnp.where(mine, key & 255, hits[0])
            total = total + jnp.where(mine, 1, 0)
        for j in range(bag):
            hits_ref[w, j] = hits[j].astype(jnp.float32)
        most = jnp.maximum(most, total)
    rows = lax.broadcasted_iota(jnp.int32, (WINDOW, lanes), 0).astype(jnp.bfloat16)
    one = jnp.ones((WINDOW, lanes), jnp.bfloat16)
    zero = jnp.zeros((WINDOW, lanes), jnp.bfloat16)

    def marks(w, j, d):
        wanted = jnp.broadcast_to(hits_ref[w, j, pl.ds(d, 1), :], (WINDOW, lanes)).astype(jnp.bfloat16)
        return jnp.where(rows == wanted, one, zero)

    def place(w, d):
        return d, pl.ds(w * WINDOW, WINDOW)

    for w in range(windows):
        for d in range(owners):
            counts = marks(w, 0, d)
            for j in range(1, STATIC_HITS):
                counts = counts + marks(w, j, d)
            out_ref[place(w, d)] = counts

    def more(j, carry):
        for w in range(windows):
            for d in range(owners):
                out_ref[place(w, d)] += marks(w, j, d)
        return carry

    lax.fori_loop(STATIC_HITS, jnp.max(most), more, 0)


def count_lookups(key_of, where, ids, rows):
    owners, bag, lanes = ids.shape
    return pl.pallas_call(
        functools.partial(count_kernel, key_of),
        grid_spec=pltpu.PrefetchScalarGridSpec(
            num_scalar_prefetch=1,
            grid=(owners // 8, rows // BLOCK),
            in_specs=[pl.BlockSpec((8 * bag, lanes), lambda g, w, s: (g, 0))],
            out_specs=pl.BlockSpec((8, BLOCK, lanes), lambda g, w, s: (g, w, 0)),
            scratch_shapes=[
                pltpu.VMEM((bag, 8, lanes), jnp.int32),
                pltpu.VMEM((BLOCK // WINDOW, bag, 8, lanes), jnp.float32),
            ],
        ),
        out_shape=jax.ShapeDtypeStruct((owners, rows, lanes), jnp.bfloat16),
        name="count",
    )(where, ids.reshape(owners * bag, lanes))


def side_by_side(w_ref, rows=slice(None)):
    return jnp.concatenate([w_ref[i, rows] for i in range(w_ref.shape[0])], axis=1)


def pool_kernel(where_ref, t0, t1, t2, t3, w_ref, out_ref):
    total = jnp.dot(t0[...], side_by_side(w_ref, slice(0, BLOCK)), preferred_element_type=jnp.float32)
    for q, t in enumerate((t1, t2, t3), 1):
        rows = slice(q * BLOCK, (q + 1) * BLOCK)
        total += jnp.dot(t[...], side_by_side(w_ref, rows), preferred_element_type=jnp.float32)
    for half in range(2):
        out_ref[half ^ (where_ref[0] & 1)] = total[:, half * 128 : (half + 1) * 128]


def pool(where, tables, counts):
    dim = tables[0].shape[0]
    owners, rows, lanes = counts.shape
    return pl.pallas_call(
        pool_kernel,
        grid_spec=pltpu.PrefetchScalarGridSpec(
            num_scalar_prefetch=1,
            grid=(owners // 2,),
            in_specs=[pl.BlockSpec(memory_space=pltpu.VMEM)] * 4
            + [pl.BlockSpec((2, rows, lanes), lambda n, s: (n, 0, 0))],
            out_specs=pl.BlockSpec((2, dim, lanes), lambda n, s: ((s[0] >> 1) ^ n, 0, 0)),
        ),
        out_shape=jax.ShapeDtypeStruct((owners, dim, lanes), jnp.float32),
        name="pool",
    )(where, *tables, counts)


def class_gradient(where_ref, w_ref, *grads):
    total = None
    for core, g in enumerate(grads):
        counts = jnp.concatenate([w_ref[core * 8 + (z ^ where_ref[0])] for z in range(8)], axis=1)
        part = jnp.dot(counts, g[...], preferred_element_type=jnp.float32)
        total = part if total is None else total + part
    return total


def gradient_kernel(where_ref, w_ref, g0, g1, out_ref):
    out_ref[...] = class_gradient(where_ref, w_ref, g0, g1)


def update_kernel(where_ref, w_ref, g0, g1, before_ref, pieces_ref, out_ref):
    gradient = before_ref[...] + class_gradient(where_ref, w_ref, g0, g1)
    for i in range(out_ref.shape[0]):
        old = pieces_ref[(8 * pl.program_id(0) + i - where_ref[2]) & 31].astype(jnp.float32)
        out_ref[i] = (old - STEP_RATE * gradient[i * PIECE : (i + 1) * PIECE]).astype(jnp.bfloat16)


def apply_counts(where, counts, grads, *more):
    owners, rows, lanes = counts.shape
    dim = grads[0].shape[1]
    tile = pl.BlockSpec((256, dim), lambda n, s: (n, 0))
    specs = [pl.BlockSpec((owners, 256, lanes), lambda n, s: (0, n, 0))]
    specs += [pl.BlockSpec(g.shape, lambda n, s: (0, 0)) for g in grads]
    if more:
        specs += [tile, pl.BlockSpec(more[1].shape, lambda n, s: (0, 0, 0))]
        out_spec = pl.BlockSpec((8, PIECE, dim), lambda n, s: (n, 0, 0))
        out_shape = jax.ShapeDtypeStruct(more[1].shape, jnp.bfloat16)
    else:
        out_spec, out_shape = tile, jax.ShapeDtypeStruct((rows, dim), jnp.float32)
    return pl.pallas_call(
        update_kernel if more else gradient_kernel,
        grid_spec=pltpu.PrefetchScalarGridSpec(
            num_scalar_prefetch=1, grid=(rows // 256,), in_specs=specs, out_specs=out_spec
        ),
        out_shape=out_shape,
        name="update" if more else "gradient",
    )(where, counts, *grads, *more)


def swap(values, axis):
    return lax.ppermute(values, axis, [(0, 1), (1, 0)])


def step(tables, indices, block_shift, pooled_grad):
    z, xl, core = (lax.axis_index(a) for a in ROW)
    shift = lax.dynamic_index_in_dim(block_shift, lax.axis_index("grp"), keepdims=False)
    where = jnp.stack([z, 2 * xl + core, shift])

    grads = lax.all_gather(pooled_grad[:, 0, :], "z", axis=0, tiled=True)

    columns = lax.all_to_all(jnp.swapaxes(tables, 1, 2), "grp", 0, 0, tiled=True).reshape(-1, BLOCK)

    ids = indices[:, 0, :].T.astype(jnp.int16)[None]
    for hop in (1, 2, 4):
        arrived = lax.ppermute(ids, "z", [(i, i ^ hop) for i in range(8)])
        ids = jnp.concatenate([ids, arrived], axis=0)
    ids = ids.astype(jnp.int32)
    both = jnp.concatenate([ids, swap(ids, "core")], axis=0)
    both_across = swap(both, "xl")

    pool_counts = count_lookups(pool_key, where, ids, 4 * BLOCK)
    across_core = swap(columns, "core")
    across_xl = swap(columns, "xl")
    across_both = swap(across_xl, "core")
    partial = pool(where, (columns, across_core, across_xl, across_both), pool_counts)
    pooled = lax.psum_scatter(partial, "z", scatter_dimension=0, tiled=True)[0]
    pooled = pooled.T.astype(jnp.bfloat16)[:, None, :]

    pieces = lax.all_to_all(columns.T.reshape(32, PIECE, -1), ROW, 0, 0, tiled=True)
    counts_own = count_lookups(update_key, where, both, BLOCK)
    counts_across = count_lookups(update_key, where, both_across, BLOCK)
    gradient = apply_counts(where, counts_own, (grads, swap(grads, "core")))
    grads = swap(grads, "xl")
    fresh = apply_counts(where, counts_across, (grads, swap(grads, "core")), gradient, pieces)
    updated = lax.all_to_all(fresh, ROW, 0, 0, tiled=True)
    return pooled, updated.reshape(1, BLOCK, -1)


def solution(mesh):
    split = Mesh(mesh.devices.reshape(8, 8, 2, 2), ("grp",) + ROW)
    return jax.shard_map(
        step,
        mesh=split,
        in_specs=(P(None, ROW, "grp"), P(ROW, "grp", None), P(), P(ROW, "grp", None)),
        out_specs=(P(ROW, "grp", None), P("grp", ROW, None)),
        check_vma=False,
    )
```

profile of v0, /device:TPU:4, one launch (start us, length us, event | category | flops | bytes accessed | tf_op | source)
XLA Modules:
  0.0 205.1 jit_solution(12698762469551998107)
XLA Ops:
  7.2 21.8 %all_to_all.15 = bf16[8,64,1024]{2,1,0:T(8,128)(2,1)S(1)} all-to-all(bf16[8,64,1024]{2,1,0:T(8,128)(2,1)} %bitcast.34), channel_id=1, replica_groups=mesh['grp'=8,'z'=8,'xl'=2,'core'=2] {'grp'}, dimensions={0} | all-to-all | bytes 2097152 | tf_op jit(solution)/shard_map/all_to_all | solution.py:180
  29.0 1.1 collective-permute-start.1
  30.3 22.4 %collective-permute-done.1.t2 = bf16[512,1024]{1,0:T(8,128)(2,1)S(1)} collective-permute-done((bf16[512,1024]{1,0:T(8,128)(2,1)S(1)}, bf16[512,1024]{1,0:T(8,128)(2,1)S(1)}, u32[]{:S(2)}, u32[]{:S(2)}) %collective-permute-start.1) | collective-permute-done | bytes 1048608 | tf_op jit(solution)/shard_map/ppermute | solution.py:170
  53.4 1.9 collective-permute-start.3
  55.3 1.8 collective-permute-done.3
  57.1 3.2 %collective-permute-start.4 = (s16[2,32,128]{2,1,0:T(8,128)(2,1)S(1)}, s16[2,32,128]{2,1,0:T(8,128)(2,1)S(1)}, u32[]{:S(2)}, u32[]{:S(2)}) collective-permute-start(s16[2,32,128]{2,1,0:T(8,128)(2,1)S(1)} %pad_add_fusion.2), channel_id=1, source_target_pairs={{0,8},{4,12},{8,0},{12,4},{16,24},{20,28},{24,16},{28,20},{1,9},{5... | collective-permute-start | bytes 49160 | tf_op jit(solution)/shard_map/ppermute | solution.py:184
  60.3 1.2 dynamic_slice.4
  62.5 6.4 %collective-permute-start.5 = (s16[4,32,128]{2,1,0:T(8,128)(2,1)S(1)}, s16[4,32,128]{2,1,0:T(8,128)(2,1)S(1)}, u32[]{:S(2)}, u32[]{:S(2)}) collective-permute-start(s16[4,32,128]{2,1,0:T(8,128)(2,1)S(1)} %pad_add_fusion.1), channel_id=1, source_target_pairs={{0,16},{4,20},{8,24},{12,28},{16,0},{20,4},{24,8},{28,12},{1,17},{... | collective-permute-start | bytes 98312 | tf_op jit(solution)/shard_map/ppermute | solution.py:184
  68.9 1.2 pad_add_fusion.3.where_ref
  71.5 9.3 %count.3.w_ref = bf16[8,4096,128]{2,1,0:T(8,128)(2,1)} custom-call(s32[3]{0:T(128)} %pad_add_fusion.3.where_ref, s32[256,128]{1,0:T(8,128)} %bitcast.29), custom_call_target="tpu_custom_call" | custom-call | tf_op jit(solution)/shard_map/count/pallas_call | solution.py:80
  81.8 10.1 %pool.1 = f32[8,512,128]{2,1,0:T(8,128)} custom-call(s32[3]{0:T(128)} %pad_add_fusion.3.where_ref, bf16[512,1024]{1,0:T(8,128)(2,1)} %bitcast.26, bf16[512,1024]{1,0:T(8,128)(2,1)} %copy-done.6, bf16[512,1024]{1,0:T(8,128)(2,1)} %copy-done.5, bf16[512,1024]{1,0:T(8,128)(2,1)} %collective-permute-done.2.t3, bf16[8,4096,128]{2,1,0:T(8,128)(2,1)} %count.3.w_ref), custom_call_target="tpu_custom_call" | custom-call | tf_op jit(solution)/shard_map/pool/pallas_call | solution.py:113
  91.9 1.3 collective-permute-start.8
  93.2 1.3 copy.6
  94.5 7.8 %all-to-all-start.1 = ((bf16[32,32,512]{2,1,0:T(8,128)(2,1)}), bf16[32,32,512]{2,1,0:T(8,128)(2,1)S(1)}, u32[]{:S(2)}, u32[]{:S(2)}) async-start(bf16[32,32,512]{2,1,0:T(8,128)(2,1)} %bitcast.17), calls=%async_computation.2 | async-start | bytes 2097152 | tf_op jit(solution)/shard_map/all_to_all | solution.py:198
  102.7 17.8 %collective-permute-done.8.g0 = bf16[1024,512]{1,0:T(8,128)(2,1)} collective-permute-done((bf16[1024,512]{1,0:T(8,128)(2,1)}, bf16[1024,512]{1,0:T(8,128)(2,1)}, u32[]{:S(2)}, u32[]{:S(2)}) %collective-permute-start.8) | collective-permute-done | bytes 1048608 | tf_op jit(solution)/shard_map/ppermute | solution.py:170
  121.0 2.5 %collective-permute-done.6 = s32[8,32,128]{2,1,0:T(8,128)S(1)} collective-permute-done((s32[8,32,128]{2,1,0:T(8,128)S(1)}, s32[8,32,128]{2,1,0:T(8,128)S(1)}, u32[]{:S(2)}, u32[]{:S(2)}) %collective-permute-start.6) | collective-permute-done | bytes 131104 | tf_op jit(solution)/shard_map/ppermute | solution.py:170
  123.6 2.1 %collective-permute-start.7 = (s32[16,32,128]{2,1,0:T(8,128)S(1)}, s32[16,32,128]{2,1,0:T(8,128)}, u32[]{:S(2)}, u32[]{:S(2)}) collective-permute-start(s32[16,32,128]{2,1,0:T(8,128)S(1)} %pad_add_fusion), channel_id=1, source_target_pairs={{0,2},{2,0},{1,3},{3,1},{4,6},{6,4},{5,7},{7,5},{8,10},{10,8},{9,1... | collective-permute-start | bytes 786440 | tf_op jit(solution)/shard_map/ppermute | solution.py:170
  125.7 7.3 %count.5.w_ref = bf16[16,1024,128]{2,1,0:T(8,128)(2,1)} custom-call(s32[3]{0:T(128)} %pad_add_fusion.3.where_ref, s32[512,128]{1,0:T(8,128)} %bitcast.33), custom_call_target="tpu_custom_call" | custom-call | tf_op jit(solution)/shard_map/count/pallas_call | solution.py:80
  132.9 3.0 %collective-permute-done.7 = s32[16,32,128]{2,1,0:T(8,128)} collective-permute-done((s32[16,32,128]{2,1,0:T(8,128)S(1)}, s32[16,32,128]{2,1,0:T(8,128)}, u32[]{:S(2)}, u32[]{:S(2)}) %collective-permute-start.7) | collective-permute-done | bytes 262176 | tf_op jit(solution)/shard_map/ppermute | solution.py:170
  135.9 7.2 %count.4.w_ref = bf16[16,1024,128]{2,1,0:T(8,128)(2,1)} custom-call(s32[3]{0:T(128)} %pad_add_fusion.3.where_ref, s32[512,128]{1,0:T(8,128)} %bitcast.13.ids_ref), custom_call_target="tpu_custom_call" | custom-call | tf_op jit(solution)/shard_map/count/pallas_call | solution.py:80
  144.1 7.0 %gradient.1.before_ref = f32[1024,512]{1,0:T(8,128)} custom-call(s32[3]{0:T(128)} %pad_add_fusion.3.where_ref, bf16[16,1024,128]{2,1,0:T(8,128)(2,1)} %count.5.w_ref, bf16[1024,512]{1,0:T(8,128)(2,1)} %bitcast.31, bf16[1024,512]{1,0:T(8,128)(2,1)} %copy-done.7), custom_call_target="tpu_custom_call" | custom-call | tf_op jit(solution)/shard_map/gradient/pallas_call | solution.py:159
  152.1 7.5 %update.1 = bf16[32,32,512]{2,1,0:T(8,128)(2,1)} custom-call(s32[3]{0:T(128)} %pad_add_fusion.3.where_ref, bf16[16,1024,128]{2,1,0:T(8,128)(2,1)} %count.4.w_ref, bf16[1024,512]{1,0:T(8,128)(2,1)} %collective-permute-done.8.g0, bf16[1024,512]{1,0:T(8,128)(2,1)} %collective-permute-done.9.g1, f32[1024,512]{1,0:T(8,128)} %gradient.1.before_ref, ...), custom_call_target="tpu_custom_call" | custom-call | tf_op jit(solution)/shard_map/update/pallas_call | solution.py:159
  159.6 36.0 %all_to_all.16 = bf16[32,32,512]{2,1,0:T(8,128)(2,1)S(1)} all-to-all(bf16[32,32,512]{2,1,0:T(8,128)(2,1)} %update.1), channel_id=1, replica_groups=mesh['grp'=8,'z'=8,'xl'=2,'core'=2] {'z','xl','core'}, dimensions={0} | all-to-all | bytes 2097152 | tf_op jit(solution)/shard_map/all_to_all | solution.py:204
  197.3 1.0 copy.9
  (43 shorter events, 8.8 us)
Async XLA Ops:
  7.2 84.7 %all-gather.3.cloned.1.call-start = ((), (), s32[]{:S(2)}) async-start(), calls=%async_computation.5 | async-start | bytes 1179648 | tf_op jit(solution)/shard_map/all_gather | solution.py:178
  29.0 51.8 %copy-start = (bf16[8,64,1024]{2,1,0:T(8,128)(2,1)}, bf16[8,64,1024]{2,1,0:T(8,128)(2,1)S(1)}, u32[]{:S(2)}) copy-start(bf16[8,64,1024]{2,1,0:T(8,128)(2,1)S(1)} %all_to_all.15) | copy-start | bytes 3145732
  29.0 23.6 %collective-permute-start.1 = (bf16[512,1024]{1,0:T(8,128)(2,1)S(1)}, bf16[512,1024]{1,0:T(8,128)(2,1)S(1)}, u32[]{:S(2)}, u32[]{:S(2)}) collective-permute-start(bf16[512,1024]{1,0:T(8,128)(2,1)S(1)} %bitcast.24), channel_id=1, source_target_pairs={{0,2},{2,0},{1,3},{3,1},{4,6},{6,4},{5,7},{7,5},{8,10},{10,8},{9,1... | collective-permute-start | bytes 3145736 | tf_op jit(solution)/shard_map/ppermute | solution.py:170
  30.1 165.4 %reduce-scatter.2.cloned.1.call-start = ((), (), s32[]{:S(2)}) async-start(), calls=%async_computation.4 | async-start | bytes 2359296 | tf_op jit(solution)/shard_map/reduce_scatter | solution.py:195
  30.2 50.6 %collective-permute-start = (bf16[512,1024]{1,0:T(8,128)(2,1)S(1)}, bf16[512,1024]{1,0:T(8,128)(2,1)S(1)}, u32[]{:S(2)}, u32[]{:S(2)}) collective-permute-start(bf16[512,1024]{1,0:T(8,128)(2,1)S(1)} %bitcast.25), channel_id=1, source_target_pairs={{0,1},{1,0},{2,3},{3,2},{4,5},{5,4},{6,7},{7,6},{8,9},{9,8},{10,11... | collective-permute-start | bytes 3145736 | tf_op jit(solution)/shard_map/ppermute | solution.py:170
  52.6 28.1 %copy-start.5 = (bf16[512,1024]{1,0:T(8,128)(2,1)}, bf16[512,1024]{1,0:T(8,128)(2,1)S(1)}, u32[]{:S(2)}) copy-start(bf16[512,1024]{1,0:T(8,128)(2,1)S(1)} %collective-permute-done.1.t2) | copy-start | bytes 3145732
  52.6 28.2 %collective-permute-start.2 = (bf16[512,1024]{1,0:T(8,128)(2,1)S(1)}, bf16[512,1024]{1,0:T(8,128)(2,1)}, u32[]{:S(2)}, u32[]{:S(2)}) collective-permute-start(bf16[512,1024]{1,0:T(8,128)(2,1)S(1)} %collective-permute-done.1.t2), channel_id=1, source_target_pairs={{0,1},{1,0},{2,3},{3,2},{4,5},{5,4},{6,7},{7,6},{8,9},{9,8},{10,11... | collective-permute-start | bytes 3145736 | tf_op jit(solution)/shard_map/ppermute | solution.py:170
  53.4 3.7 %collective-permute-start.3 = (s16[1,32,128]{2,1,0:T(8,128)(2,1)S(1)}, s16[1,32,128]{2,1,0:T(8,128)(2,1)S(1)}, u32[]{:S(2)}, u32[]{:S(2)}) collective-permute-start(s16[1,32,128]{2,1,0:T(8,128)(2,1)S(1)} %convert_bitcast_fusion.1), channel_id=1, source_target_pairs={{0,4},{4,0},{8,12},{12,8},{16,20},{20,16},{24,28},{28,24},{1,5},{5... | collective-permute-start | bytes 24584 | tf_op jit(solution)/shard_map/ppermute | solution.py:184
  57.1 5.4 %collective-permute-start.4 = (s16[2,32,128]{2,1,0:T(8,128)(2,1)S(1)}, s16[2,32,128]{2,1,0:T(8,128)(2,1)S(1)}, u32[]{:S(2)}, u32[]{:S(2)}) collective-permute-start(s16[2,32,128]{2,1,0:T(8,128)(2,1)S(1)} %pad_add_fusion.2), channel_id=1, source_target_pairs={{0,8},{4,12},{8,0},{12,4},{16,24},{20,28},{24,16},{28,20},{1,9},{5... | collective-permute-start | bytes 49160 | tf_op jit(solution)/shard_map/ppermute | solution.py:184
  62.5 8.4 %collective-permute-start.5 = (s16[4,32,128]{2,1,0:T(8,128)(2,1)S(1)}, s16[4,32,128]{2,1,0:T(8,128)(2,1)S(1)}, u32[]{:S(2)}, u32[]{:S(2)}) collective-permute-start(s16[4,32,128]{2,1,0:T(8,128)(2,1)S(1)} %pad_add_fusion.1), channel_id=1, source_target_pairs={{0,16},{4,20},{8,24},{12,28},{16,0},{20,4},{24,8},{28,12},{1,17},{... | collective-permute-start | bytes 98312 | tf_op jit(solution)/shard_map/ppermute | solution.py:184
  80.8 1.0 copy-start.6
  80.8 12.4 %copy-start.1 = (bf16[8,64,1024]{2,1,0:T(8,128)(2,1)S(1)}, bf16[8,64,1024]{2,1,0:T(8,128)(2,1)}, u32[]{:S(2)}) copy-start(bf16[8,64,1024]{2,1,0:T(8,128)(2,1)} %copy-done) | copy-start | bytes 3145732
  91.8 28.6 %copy-start.3 = (s32[8,32,128]{2,1,0:T(8,128)S(1)}, s32[8,32,128]{2,1,0:T(8,128)}, u32[]{:S(2)}) copy-start(s32[8,32,128]{2,1,0:T(8,128)} %add_convert_fusion) | copy-start | bytes 393220
  91.9 10.4 %copy-start.4 = (bf16[1024,1,512]{2,0,1:T(8,128)(2,1)S(1)}, bf16[1024,1,512]{2,0,1:T(8,128)(2,1)}, u32[]{:S(2)}) copy-start(bf16[1024,1,512]{2,0,1:T(8,128)(2,1)} %all-gather.3.cloned.1.call-done) | copy-start | bytes 3145732
  91.9 28.6 %collective-permute-start.8 = (bf16[1024,512]{1,0:T(8,128)(2,1)}, bf16[1024,512]{1,0:T(8,128)(2,1)}, u32[]{:S(2)}, u32[]{:S(2)}) collective-permute-start(bf16[1024,512]{1,0:T(8,128)(2,1)} %bitcast.30), channel_id=1, source_target_pairs={{0,2},{2,0},{1,3},{3,1},{4,6},{6,4},{5,7},{7,5},{8,10},{10,8},{9,1... | collective-permute-start | bytes 3145736 | tf_op jit(solution)/shard_map/ppermute | solution.py:170
  94.5 56.6 %all-to-all-start.1 = ((bf16[32,32,512]{2,1,0:T(8,128)(2,1)}), bf16[32,32,512]{2,1,0:T(8,128)(2,1)S(1)}, u32[]{:S(2)}, u32[]{:S(2)}) async-start(bf16[32,32,512]{2,1,0:T(8,128)(2,1)} %bitcast.17), calls=%async_computation.2 | async-start | bytes 2097152 | tf_op jit(solution)/shard_map/all_to_all | solution.py:198
  102.3 40.8 %collective-permute-start.10 = (bf16[1024,512]{1,0:T(8,128)(2,1)S(1)}, bf16[1024,512]{1,0:T(8,128)(2,1)S(1)}, u32[]{:S(2)}, u32[]{:S(2)}) collective-permute-start(bf16[1024,512]{1,0:T(8,128)(2,1)S(1)} %bitcast.32), channel_id=1, source_target_pairs={{0,1},{1,0},{2,3},{3,2},{4,5},{5,4},{6,7},{7,6},{8,9},{9,8},{10,11... | collective-permute-start | bytes 3145736 | tf_op jit(solution)/shard_map/ppermute | solution.py:170
  120.5 30.6 %collective-permute-start.9 = (bf16[1024,512]{1,0:T(8,128)(2,1)}, bf16[1024,512]{1,0:T(8,128)(2,1)}, u32[]{:S(2)}, u32[]{:S(2)}) collective-permute-start(bf16[1024,512]{1,0:T(8,128)(2,1)} %collective-permute-done.8.g0), channel_id=1, source_target_pairs={{0,1},{1,0},{2,3},{3,2},{4,5},{5,4},{6,7},{7,6},{8,9},{9,8},{10,11... | collective-permute-start | bytes 3145736 | tf_op jit(solution)/shard_map/ppermute | solution.py:170
  120.5 3.1 %collective-permute-start.6 = (s32[8,32,128]{2,1,0:T(8,128)S(1)}, s32[8,32,128]{2,1,0:T(8,128)S(1)}, u32[]{:S(2)}, u32[]{:S(2)}) collective-permute-start(s32[8,32,128]{2,1,0:T(8,128)S(1)} %copy-done.3), channel_id=1, source_target_pairs={{0,1},{1,0},{2,3},{3,2},{4,5},{5,4},{6,7},{7,6},{8,9},{9,8},{10,11... | collective-permute-start | bytes 393224 | tf_op jit(solution)/shard_map/ppermute | solution.py:170
  123.6 2.1 %copy-start.8 = (s32[16,32,128]{2,1,0:T(8,128)}, s32[16,32,128]{2,1,0:T(8,128)S(1)}, u32[]{:S(2)}) copy-start(s32[16,32,128]{2,1,0:T(8,128)S(1)} %pad_add_fusion) | copy-start | bytes 786436
  123.6 12.3 %collective-permute-start.7 = (s32[16,32,128]{2,1,0:T(8,128)S(1)}, s32[16,32,128]{2,1,0:T(8,128)}, u32[]{:S(2)}, u32[]{:S(2)}) collective-permute-start(s32[16,32,128]{2,1,0:T(8,128)S(1)} %pad_add_fusion), channel_id=1, source_target_pairs={{0,2},{2,0},{1,3},{3,1},{4,6},{6,4},{5,7},{7,5},{8,10},{10,8},{9,1... | collective-permute-start | bytes 786440 | tf_op jit(solution)/shard_map/ppermute | solution.py:170
  143.1 1.0 copy-start.7
  151.1 1.0 copy-start.2
Sparse Core Ops, SparseCore 0:
  30.2 39.5 all-gather.2
  92.0 60.5 reduce-scatter.1
where the time goes:
time: 208 us; the launch traced here: 205 us
  blocking collectives  57.8 us (28%)
  waiting for transfers between devices  49.1 us (24%)
  Pallas kernels  48.3 us (23%)
  starting transfers between devices  24.9 us (12%)
  between operations  14.1 us (7%)
  local copies, waits for them, and re-layouts  7.2 us (3%)
  other arithmetic  3.62 us (2%)
    ppermute x8, waiting for transfers between devices, swap(): return lax.ppermute(values, axis, [(0, 1), (1, 0)])  45.7 us
    all_to_all x1, blocking collectives, step(): updated = lax.all_to_all(fresh, ROW, 0, 0, tiled=True)  36 us
    pallas_call x3, Pallas kernels, count_lookups(): pl.pallas_call(functools.partial(count_kernel, key_of), grid_spec=pltpu.P...  23.7 us
    all_to_all x1, blocking collectives, step(): lax.all_to_all(jnp.swapaxes(tables, 1, 2), 'grp', 0, 0, tiled=True)  21.8 us
    pallas_call x2, Pallas kernels, apply_counts(): pl.pallas_call(update_kernel if more else gradient_kernel, grid_spec=pltp...  14.5 us
    ppermute x3, starting transfers between devices, step(): arrived = lax.ppermute(ids, 'z', [(i, i ^ hop) for i in range(8)])  11.6 us
    pallas_call x1, Pallas kernels, pool(): pl.pallas_call(pool_kernel, grid_spec=pltpu.PrefetchScalarGridSpec(num_sc...  10.1 us
    all_to_all x1, starting transfers between devices, step(): lax.all_to_all(columns.T.reshape(32, PIECE, -1), ROW, 0, 0, tiled=True)  7.82 us
  transfers between devices with their start and end apart: 14, of which 7 were waited for; matrix products, arithmetic and copies ran while one was open for 3% of the time, Pallas kernels for 24%

commit v1 on v0

--- a/solution.py
+++ b/solution.py
@@ -124,46 +124,30 @@
     )(where, *tables, counts)
 
 
-def class_gradient(where_ref, w_ref, *grads):
-    total = None
-    for core, g in enumerate(grads):
-        counts = jnp.concatenate([w_ref[core * 8 + (z ^ where_ref[0])] for z in range(8)], axis=1)
-        part = jnp.dot(counts, g[...], preferred_element_type=jnp.float32)
-        total = part if total is None else total + part
-    return total
-
-
-def gradient_kernel(where_ref, w_ref, g0, g1, out_ref):
-    out_ref[...] = class_gradient(where_ref, w_ref, g0, g1)
-
-
-def update_kernel(where_ref, w_ref, g0, g1, before_ref, pieces_ref, out_ref):
-    gradient = before_ref[...] + class_gradient(where_ref, w_ref, g0, g1)
+def update_kernel(where_ref, w_own, w_across, grads_ref, pieces_ref, out_ref):
+    order = [((c ^ (where_ref[1] & 1)) * 8 + (z ^ where_ref[0])) for z in range(8) for c in range(2)]
+    counts = jnp.concatenate([w[i] for i in order for w in (w_own, w_across)], axis=1)
+    gradient = jnp.dot(counts, grads_ref[...], preferred_element_type=jnp.float32)
     for i in range(out_ref.shape[0]):
         old = pieces_ref[(8 * pl.program_id(0) + i - where_ref[2]) & 31].astype(jnp.float32)
         out_ref[i] = (old - STEP_RATE * gradient[i * PIECE : (i + 1) * PIECE]).astype(jnp.bfloat16)
 
 
-def apply_counts(where, counts, grads, *more):
-    owners, rows, lanes = counts.shape
-    dim = grads[0].shape[1]
-    tile = pl.BlockSpec((256, dim), lambda n, s: (n, 0))
-    specs = [pl.BlockSpec((owners, 256, lanes), lambda n, s: (0, n, 0))]
-    specs += [pl.BlockSpec(g.shape, lambda n, s: (0, 0)) for g in grads]
-    if more:
-        specs += [tile, pl.BlockSpec(more[1].shape, lambda n, s: (0, 0, 0))]
-        out_spec = pl.BlockSpec((8, PIECE, dim), lambda n, s: (n, 0, 0))
-        out_shape = jax.ShapeDtypeStruct(more[1].shape, jnp.bfloat16)
-    else:
-        out_spec, out_shape = tile, jax.ShapeDtypeStruct((rows, dim), jnp.float32)
+def update(where, counts, grads, pieces):
+    owners, rows, lanes = counts[0].shape
+    dim = grads.shape[1]
     return pl.pallas_call(
-        update_kernel if more else gradient_kernel,
+        update_kernel,
         grid_spec=pltpu.PrefetchScalarGridSpec(
-            num_scalar_prefetch=1, grid=(rows // 256,), in_specs=specs, out_specs=out_spec
+            num_scalar_prefetch=1,
+            grid=(rows // 256,),
+            in_specs=[pl.BlockSpec((owners, 256, lanes), lambda n, s: (0, n, 0))] * 2
+            + [pl.BlockSpec(grads.shape, lambda n, s: (0, 0)), pl.BlockSpec(pieces.shape, lambda n, s: (0, 0, 0))],
+            out_specs=pl.BlockSpec((8, PIECE, dim), lambda n, s: (n, 0, 0)),
         ),
-        out_shape=out_shape,
-        name="update" if more else "gradient",
-    )(where, counts, *grads, *more)
+        out_shape=jax.ShapeDtypeStruct(pieces.shape, jnp.bfloat16),
+        name="update",
+    )(where, *counts, grads, pieces)
 
 
 def swap(values, axis):
@@ -175,7 +159,10 @@
     shift = lax.dynamic_index_in_dim(block_shift, lax.axis_index("grp"), keepdims=False)
     where = jnp.stack([z, 2 * xl + core, shift])
 
-    grads = lax.all_gather(pooled_grad[:, 0, :], "z", axis=0, tiled=True)
+    own = pooled_grad[:, 0, :]
+    across = swap(own, "xl")
+    own = jnp.concatenate([own, across], axis=0)
+    grads = lax.all_gather(own, ("z", "core"), axis=0, tiled=True)
 
     columns = lax.all_to_all(jnp.swapaxes(tables, 1, 2), "grp", 0, 0, tiled=True).reshape(-1, BLOCK)
 
@@ -198,9 +185,7 @@
     pieces = lax.all_to_all(columns.T.reshape(32, PIECE, -1), ROW, 0, 0, tiled=True)
     counts_own = count_lookups(update_key, where, both, BLOCK)
     counts_across = count_lookups(update_key, where, both_across, BLOCK)
-    gradient = apply_counts(where, counts_own, (grads, swap(grads, "core")))
-    grads = swap(grads, "xl")
-    fresh = apply_counts(where, counts_across, (grads, swap(grads, "core")), gradient, pieces)
+    fresh = update(where, (counts_own, counts_across), grads, pieces)
     updated = lax.all_to_all(fresh, ROW, 0, 0, tiled=True)
     return pooled, updated.reshape(1, BLOCK, -1)
 

time: 208 us -> 202 us (0.971)
  blocking collectives: 57.8 us -> 20.8 us
  waiting for transfers between devices: 49.1 us -> 76.8 us
  Pallas kernels: 48.3 us -> 43.9 us
  starting transfers between devices: 24.9 us -> 29.2 us
    all_to_all x1 -> x0, blocking collectives: 36 us -> none  [step(): updated = lax.all_to_all(fresh, ROW, 0, 0, tiled=True)]
    all_to_all x0 -> x1, waiting for transfers between devices: none -> 26.8 us  [step(): updated = lax.all_to_all(fresh, ROW, 0, 0, tiled=True)]
    all_to_all x1, waiting for transfers between devices: 0.01 us -> 17.8 us  [step(): lax.all_to_all(columns.T.reshape(32, PIECE, -1), ROW, 0, 0, tiled=True)]
    ppermute x8 -> x6, waiting for transfers between devices: 45.7 us -> 29.2 us  [swap(): return lax.ppermute(values, axis, [(0, 1), (1, 0)])]
    pallas_call x2 -> x1, Pallas kernels: 14.5 us -> 10.1 us  [update(): pl.pallas_call(update_kernel, grid_spec=pltpu.PrefetchScalarGridSpec(num_...]
    all_to_all x0 -> x1, starting transfers between devices: none -> 4.01 us  [step(): updated = lax.all_to_all(fresh, ROW, 0, 0, tiled=True)]
    ppermute x8 -> x6, starting transfers between devices: 5.41 us -> 4.9 us  [swap(): return lax.ppermute(values, axis, [(0, 1), (1, 0)])]
    unnamed x20 -> x18, local copies, waits for them, and re-layouts: 4.66 us -> 4.4 us
  transfers between devices with their start and end apart: 14 -> 13, of which waited for: 7 -> 9; matrix products, arithmetic and copies ran while one was open for 3% -> 4% of each run, Pallas kernels for 24% -> 22%
where the time goes in v1:
time: 202 us; the launch traced here: 199 us
  waiting for transfers between devices  76.8 us (38%)
  Pallas kernels  43.9 us (22%)
  starting transfers between devices  29.2 us (14%)
  blocking collectives  20.8 us (10%)
  between operations  15.6 us (8%)
  local copies, waits for them, and re-layouts  6.96 us (3%)
  other arithmetic  5.26 us (3%)
    ppermute x6, waiting for transfers between devices, swap(): return lax.ppermute(values, axis, [(0, 1), (1, 0)])  29.2 us
    all_to_all x1, waiting for transfers between devices, step(): updated = lax.all_to_all(fresh, ROW, 0, 0, tiled=True)  26.8 us
    pallas_call x3, Pallas kernels, count_lookups(): pl.pallas_call(functools.partial(count_kernel, key_of), grid_spec=pltpu.P...  23.7 us
    all_to_all x1, blocking collectives, step(): lax.all_to_all(jnp.swapaxes(tables, 1, 2), 'grp', 0, 0, tiled=True)  20.8 us
    all_to_all x1, waiting for transfers between devices, step(): lax.all_to_all(columns.T.reshape(32, PIECE, -1), ROW, 0, 0, tiled=True)  17.8 us
    ppermute x3, starting transfers between devices, step(): arrived = lax.ppermute(ids, 'z', [(i, i ^ hop) for i in range(8)])  12 us
    pallas_call x1, Pallas kernels, update(): pl.pallas_call(update_kernel, grid_spec=pltpu.PrefetchScalarGridSpec(num_...  10.1 us
    pallas_call x1, Pallas kernels, pool(): pl.pallas_call(pool_kernel, grid_spec=pltpu.PrefetchScalarGridSpec(num_sc...  10.1 us
  transfers between devices with their start and end apart: 13, of which 9 were waited for; matrix products, arithmetic and copies ran while one was open for 4% of the time, Pallas kernels for 22%

profile of v1, /device:TPU:4, one launch (start us, length us, event | category | flops | bytes accessed | tf_op | source)
XLA Modules:
  0.0 198.5 jit_solution(628705938244839219)
XLA Ops:
  8.0 1.3 collective-permute-start.8
  9.3 4.2 %collective-permute-done.8 = bf16[128,512]{1,0:T(8,128)(2,1)S(1)} collective-permute-done((bf16[128,512]{1,0:T(8,128)(2,1)}, bf16[128,512]{1,0:T(8,128)(2,1)S(1)}, u32[]{:S(2)}, u32[]{:S(2)}) %collective-permute-start.8) | collective-permute-done | bytes 131104 | tf_op jit(solution)/shard_map/ppermute | solution.py:154
  13.6 1.6 pad_maximum_fusion
  15.3 20.8 %all_to_all.15 = bf16[8,64,1024]{2,1,0:T(8,128)(2,1)S(1)} all-to-all(bf16[8,64,1024]{2,1,0:T(8,128)(2,1)} %bitcast.31), channel_id=1, replica_groups=mesh['grp'=8,'z'=8,'xl'=2,'core'=2] {'grp'}, dimensions={0} | all-to-all | bytes 2097152 | tf_op jit(solution)/shard_map/all_to_all | solution.py:167
  36.1 1.2 collective-permute-start.1
  37.3 21.2 %collective-permute-done.1.t2 = bf16[512,1024]{1,0:T(8,128)(2,1)S(1)} collective-permute-done((bf16[512,1024]{1,0:T(8,128)(2,1)S(1)}, bf16[512,1024]{1,0:T(8,128)(2,1)S(1)}, u32[]{:S(2)}, u32[]{:S(2)}) %collective-permute-start.1) | collective-permute-done | bytes 1048608 | tf_op jit(solution)/shard_map/ppermute | solution.py:154
  59.2 1.9 collective-permute-start.3
  61.2 1.7 collective-permute-done.3
  62.9 3.3 %collective-permute-start.4 = (s16[2,32,128]{2,1,0:T(8,128)(2,1)S(1)}, s16[2,32,128]{2,1,0:T(8,128)(2,1)S(1)}, u32[]{:S(2)}, u32[]{:S(2)}) collective-permute-start(s16[2,32,128]{2,1,0:T(8,128)(2,1)S(1)} %pad_add_fusion.2), channel_id=1, source_target_pairs={{0,8},{4,12},{8,0},{12,4},{16,24},{20,28},{24,16},{28,20},{1,9},{5... | collective-permute-start | bytes 49160 | tf_op jit(solution)/shard_map/ppermute | solution.py:171
  66.2 1.2 dynamic_slice.4
  67.9 6.8 %collective-permute-start.5 = (s16[4,32,128]{2,1,0:T(8,128)(2,1)S(1)}, s16[4,32,128]{2,1,0:T(8,128)(2,1)S(1)}, u32[]{:S(2)}, u32[]{:S(2)}) collective-permute-start(s16[4,32,128]{2,1,0:T(8,128)(2,1)S(1)} %pad_add_fusion.1), channel_id=1, source_target_pairs={{0,16},{4,20},{8,24},{12,28},{16,0},{20,4},{24,8},{28,12},{1,17},{... | collective-permute-start | bytes 98312 | tf_op jit(solution)/shard_map/ppermute | solution.py:171
  74.7 1.3 pad_add_fusion.3.where_ref
  77.3 9.3 %count.3.w_ref = bf16[8,4096,128]{2,1,0:T(8,128)(2,1)} custom-call(s32[3]{0:T(128)} %pad_add_fusion.3.where_ref, s32[256,128]{1,0:T(8,128)} %bitcast.29), custom_call_target="tpu_custom_call" | custom-call | tf_op jit(solution)/shard_map/count/pallas_call | solution.py:80
  87.6 10.1 %pool.1 = f32[8,512,128]{2,1,0:T(8,128)} custom-call(s32[3]{0:T(128)} %pad_add_fusion.3.where_ref, bf16[512,1024]{1,0:T(8,128)(2,1)} %bitcast.26, bf16[512,1024]{1,0:T(8,128)(2,1)} %copy-done.5, bf16[512,1024]{1,0:T(8,128)(2,1)} %copy-done.4, bf16[512,1024]{1,0:T(8,128)(2,1)} %collective-permute-done.2.t3, bf16[8,4096,128]{2,1,0:T(8,128)(2,1)} %count.3.w_ref), custom_call_target="tpu_custom_call" | custom-call | tf_op jit(solution)/shard_map/pool/pallas_call | solution.py:113
  97.7 1.3 copy.6
  99.0 8.2 %all-to-all-start.1 = ((bf16[32,32,512]{2,1,0:T(8,128)(2,1)}), bf16[32,32,512]{2,1,0:T(8,128)(2,1)S(1)}, u32[]{:S(2)}, u32[]{:S(2)}) async-start(bf16[32,32,512]{2,1,0:T(8,128)(2,1)} %bitcast.17), calls=%async_computation.2 | async-start | bytes 2097152 | tf_op jit(solution)/shard_map/all_to_all | solution.py:185
  108.7 2.1 %collective-permute-start.7 = (s32[16,32,128]{2,1,0:T(8,128)S(1)}, s32[16,32,128]{2,1,0:T(8,128)S(1)}, u32[]{:S(2)}, u32[]{:S(2)}) collective-permute-start(s32[16,32,128]{2,1,0:T(8,128)S(1)} %pad_add_fusion), channel_id=1, source_target_pairs={{0,2},{2,0},{1,3},{3,1},{4,6},{6,4},{5,7},{7,5},{8,10},{10,8},{9,1... | collective-permute-start | bytes 786440 | tf_op jit(solution)/shard_map/ppermute | solution.py:154
  110.7 7.2 %count.4.w_own = bf16[16,1024,128]{2,1,0:T(8,128)(2,1)} custom-call(s32[3]{0:T(128)} %pad_add_fusion.3.where_ref, s32[512,128]{1,0:T(8,128)} %bitcast.30), custom_call_target="tpu_custom_call" | custom-call | tf_op jit(solution)/shard_map/count/pallas_call | solution.py:80
  117.9 2.7 %collective-permute-done.7 = s32[16,32,128]{2,1,0:T(8,128)S(1)} collective-permute-done((s32[16,32,128]{2,1,0:T(8,128)S(1)}, s32[16,32,128]{2,1,0:T(8,128)S(1)}, u32[]{:S(2)}, u32[]{:S(2)}) %collective-permute-start.7) | collective-permute-done | bytes 262176 | tf_op jit(solution)/shard_map/ppermute | solution.py:154
  121.3 7.3 %count.5.w_across = bf16[16,1024,128]{2,1,0:T(8,128)(2,1)} custom-call(s32[3]{0:T(128)} %pad_add_fusion.3.where_ref, s32[512,128]{1,0:T(8,128)} %bitcast.32), custom_call_target="tpu_custom_call" | custom-call | tf_op jit(solution)/shard_map/count/pallas_call | solution.py:80
  128.6 17.8 %all-to-all-done.1.pieces_ref = bf16[32,32,512]{2,1,0:T(8,128)(2,1)S(1)} async-done(((bf16[32,32,512]{2,1,0:T(8,128)(2,1)}), bf16[32,32,512]{2,1,0:T(8,128)(2,1)S(1)}, u32[]{:S(2)}, u32[]{:S(2)}) %all-to-all-start.1) | async-done | bytes 1048608 | tf_op jit(solution)/shard_map/all_to_all | solution.py:185
  147.4 10.1 %update.1 = bf16[32,32,512]{2,1,0:T(8,128)(2,1)} custom-call(s32[3]{0:T(128)} %pad_add_fusion.3.where_ref, bf16[16,1024,128]{2,1,0:T(8,128)(2,1)} %count.4.w_own, bf16[16,1024,128]{2,1,0:T(8,128)(2,1)} %count.5.w_across, bf16[4096,512]{1,0:T(8,128)(2,1)} %all-gather.2.cloned.1.call-done.grads_ref, bf16[32,32,512]{2,1,0:T(8,128)(2,1)} %copy-done.2), custom_call_target="tpu_custom_call" | custom-call | tf_op jit(solution)/shard_map/update/pallas_call | solution.py:139
  157.5 4.0 %all-to-all-start.2 = ((bf16[32,32,512]{2,1,0:T(8,128)(2,1)}), bf16[32,32,512]{2,1,0:T(8,128)(2,1)S(1)}, u32[]{:S(2)}, u32[]{:S(2)}) async-start(bf16[32,32,512]{2,1,0:T(8,128)(2,1)} %update.1), calls=%async_computation.3 | async-start | bytes 2097152 | tf_op jit(solution)/shard_map/all_to_all | solution.py:189
  163.3 26.8 %all-to-all-done.2 = bf16[32,32,512]{2,1,0:T(8,128)(2,1)S(1)} async-done(((bf16[32,32,512]{2,1,0:T(8,128)(2,1)}), bf16[32,32,512]{2,1,0:T(8,128)(2,1)S(1)}, u32[]{:S(2)}, u32[]{:S(2)}) %all-to-all-start.2) | async-done | bytes 1048608 | tf_op jit(solution)/shard_map/all_to_all | solution.py:189
  (38 shorter events, 9.5 us)
Async XLA Ops:
  8.0 138.4 %all-gather.2.cloned.1.call-start = ((), (), s32[]{:S(2)}) async-start(), calls=%async_computation.5 | async-start | bytes 4456448 | tf_op jit(solution)/shard_map/all_gather | solution.py:165
  8.0 5.5 %collective-permute-start.8 = (bf16[128,512]{1,0:T(8,128)(2,1)}, bf16[128,512]{1,0:T(8,128)(2,1)S(1)}, u32[]{:S(2)}, u32[]{:S(2)}) collective-permute-start(bf16[128,512]{1,0:T(8,128)(2,1)} %bitcast.33), channel_id=1, source_target_pairs={{0,2},{2,0},{1,3},{3,1},{4,6},{6,4},{5,7},{7,5},{8,10},{10,8},{9,1... | collective-permute-start | bytes 393224 | tf_op jit(solution)/shard_map/ppermute | solution.py:154
  15.2 146.3 %reduce-scatter.2.cloned.1.call-start = ((), (), s32[]{:S(2)}) async-start(), calls=%async_computation.4 | async-start | bytes 2359296 | tf_op jit(solution)/shard_map/reduce_scatter | solution.py:182
  36.1 50.4 %copy-start = (bf16[8,64,1024]{2,1,0:T(8,128)(2,1)}, bf16[8,64,1024]{2,1,0:T(8,128)(2,1)S(1)}, u32[]{:S(2)}) copy-start(bf16[8,64,1024]{2,1,0:T(8,128)(2,1)S(1)} %all_to_all.15) | copy-start | bytes 3145732
  36.1 22.4 %collective-permute-start.1 = (bf16[512,1024]{1,0:T(8,128)(2,1)S(1)}, bf16[512,1024]{1,0:T(8,128)(2,1)S(1)}, u32[]{:S(2)}, u32[]{:S(2)}) collective-permute-start(bf16[512,1024]{1,0:T(8,128)(2,1)S(1)} %bitcast.24), channel_id=1, source_target_pairs={{0,2},{2,0},{1,3},{3,1},{4,6},{6,4},{5,7},{7,5},{8,10},{10,8},{9,1... | collective-permute-start | bytes 3145736 | tf_op jit(solution)/shard_map/ppermute | solution.py:154
  37.3 49.3 %collective-permute-start = (bf16[512,1024]{1,0:T(8,128)(2,1)S(1)}, bf16[512,1024]{1,0:T(8,128)(2,1)S(1)}, u32[]{:S(2)}, u32[]{:S(2)}) collective-permute-start(bf16[512,1024]{1,0:T(8,128)(2,1)S(1)} %bitcast.25), channel_id=1, source_target_pairs={{0,1},{1,0},{2,3},{3,2},{4,5},{5,4},{6,7},{7,6},{8,9},{9,8},{10,11... | collective-permute-start | bytes 3145736 | tf_op jit(solution)/shard_map/ppermute | solution.py:154
  58.5 28.0 %copy-start.4 = (bf16[512,1024]{1,0:T(8,128)(2,1)}, bf16[512,1024]{1,0:T(8,128)(2,1)S(1)}, u32[]{:S(2)}) copy-start(bf16[512,1024]{1,0:T(8,128)(2,1)S(1)} %collective-permute-done.1.t2) | copy-start | bytes 3145732
  58.5 28.1 %collective-permute-start.2 = (bf16[512,1024]{1,0:T(8,128)(2,1)S(1)}, bf16[512,1024]{1,0:T(8,128)(2,1)}, u32[]{:S(2)}, u32[]{:S(2)}) collective-permute-start(bf16[512,1024]{1,0:T(8,128)(2,1)S(1)} %collective-permute-done.1.t2), channel_id=1, source_target_pairs={{0,1},{1,0},{2,3},{3,2},{4,5},{5,4},{6,7},{7,6},{8,9},{9,8},{10,11... | collective-permute-start | bytes 3145736 | tf_op jit(solution)/shard_map/ppermute | solution.py:154
  59.2 3.7 %collective-permute-start.3 = (s16[1,32,128]{2,1,0:T(8,128)(2,1)S(1)}, s16[1,32,128]{2,1,0:T(8,128)(2,1)S(1)}, u32[]{:S(2)}, u32[]{:S(2)}) collective-permute-start(s16[1,32,128]{2,1,0:T(8,128)(2,1)S(1)} %convert_bitcast_fusion.1), channel_id=1, source_target_pairs={{0,4},{4,0},{8,12},{12,8},{16,20},{20,16},{24,28},{28,24},{1,5},{5... | collective-permute-start | bytes 24584 | tf_op jit(solution)/shard_map/ppermute | solution.py:171
  62.9 5.0 %collective-permute-start.4 = (s16[2,32,128]{2,1,0:T(8,128)(2,1)S(1)}, s16[2,32,128]{2,1,0:T(8,128)(2,1)S(1)}, u32[]{:S(2)}, u32[]{:S(2)}) collective-permute-start(s16[2,32,128]{2,1,0:T(8,128)(2,1)S(1)} %pad_add_fusion.2), channel_id=1, source_target_pairs={{0,8},{4,12},{8,0},{12,4},{16,24},{20,28},{24,16},{28,20},{1,9},{5... | collective-permute-start | bytes 49160 | tf_op jit(solution)/shard_map/ppermute | solution.py:171
  67.9 8.7 %collective-permute-start.5 = (s16[4,32,128]{2,1,0:T(8,128)(2,1)S(1)}, s16[4,32,128]{2,1,0:T(8,128)(2,1)S(1)}, u32[]{:S(2)}, u32[]{:S(2)}) collective-permute-start(s16[4,32,128]{2,1,0:T(8,128)(2,1)S(1)} %pad_add_fusion.1), channel_id=1, source_target_pairs={{0,16},{4,20},{8,24},{12,28},{16,0},{20,4},{24,8},{28,12},{1,17},{... | collective-permute-start | bytes 98312 | tf_op jit(solution)/shard_map/ppermute | solution.py:171
  86.6 1.0 copy-start.5
  86.6 11.1 %copy-start.1 = (bf16[8,64,1024]{2,1,0:T(8,128)(2,1)S(1)}, bf16[8,64,1024]{2,1,0:T(8,128)(2,1)}, u32[]{:S(2)}) copy-start(bf16[8,64,1024]{2,1,0:T(8,128)(2,1)} %copy-done) | copy-start | bytes 3145732
  97.6 9.6 %copy-start.3 = (s32[8,32,128]{2,1,0:T(8,128)S(1)}, s32[8,32,128]{2,1,0:T(8,128)}, u32[]{:S(2)}) copy-start(s32[8,32,128]{2,1,0:T(8,128)} %add_convert_fusion) | copy-start | bytes 393220
  99.0 47.4 %all-to-all-start.1 = ((bf16[32,32,512]{2,1,0:T(8,128)(2,1)}), bf16[32,32,512]{2,1,0:T(8,128)(2,1)S(1)}, u32[]{:S(2)}, u32[]{:S(2)}) async-start(bf16[32,32,512]{2,1,0:T(8,128)(2,1)} %bitcast.17), calls=%async_computation.2 | async-start | bytes 2097152 | tf_op jit(solution)/shard_map/all_to_all | solution.py:185
  107.2 1.4 collective-permute-start.6
  108.7 2.1 %copy-start.6 = (s32[16,32,128]{2,1,0:T(8,128)}, s32[16,32,128]{2,1,0:T(8,128)S(1)}, u32[]{:S(2)}) copy-start(s32[16,32,128]{2,1,0:T(8,128)S(1)} %pad_add_fusion) | copy-start | bytes 786436
  108.7 11.9 %collective-permute-start.7 = (s32[16,32,128]{2,1,0:T(8,128)S(1)}, s32[16,32,128]{2,1,0:T(8,128)S(1)}, u32[]{:S(2)}, u32[]{:S(2)}) collective-permute-start(s32[16,32,128]{2,1,0:T(8,128)S(1)} %pad_add_fusion), channel_id=1, source_target_pairs={{0,2},{2,0},{1,3},{3,1},{4,6},{6,4},{5,7},{7,5},{8,10},{10,8},{9,1... | collective-permute-start | bytes 786440 | tf_op jit(solution)/shard_map/ppermute | solution.py:154
  120.6 0.7 copy-start.7
  146.4 1.0 copy-start.2
  157.5 32.6 %all-to-all-start.2 = ((bf16[32,32,512]{2,1,0:T(8,128)(2,1)}), bf16[32,32,512]{2,1,0:T(8,128)(2,1)S(1)}, u32[]{:S(2)}, u32[]{:S(2)}) async-start(bf16[32,32,512]{2,1,0:T(8,128)(2,1)} %update.1), calls=%async_computation.3 | async-start | bytes 2097152 | tf_op jit(solution)/shard_map/all_to_all | solution.py:189
Sparse Core Ops, SparseCore 0:
  15.3 44.9 all-gather.1
Sparse Core Ops, SparseCore 1:
  97.7 59.6 reduce-scatter.1
